TPU v7x, 256 devices: a whole 4x4x8 slice. The times are simulated.
256 devices in a mesh: wide: 16 (over y_hi, x, core), blk: 16 (over y_lo, z).
Axes of the slice: x: 4, y: 4 (y_hi: 2, y_lo: 2; y = y_hi * 2 + y_lo), z: 8, core: 2. Of those that a mesh axis runs over, the one named last changes fastest.
Arguments:
- features: bfloat16 [2048, 768], P('blk'), may hold values from -6 to 6
- weights: bfloat16 [262144, 768], P(('wide', 'blk')), may hold values from -0.21875 to 0.21875
- momentum: bfloat16 [262144, 768], P(('wide', 'blk')), may hold values from -48 to 48
- targets: bfloat16 [2048, 262144], P(None, ('wide', 'blk')), may hold values from 0 to 1
Outputs:
- new_weights: bfloat16 [262144, 768], P(('wide', 'blk'))
- new_momentum: bfloat16 [262144, 768], P(('wide', 'blk'))
- feature_grad: bfloat16 [2048, 768], P('blk', 'wide')
All inputs are finite; a program needn't handle non-finite values.
Results may differ from a plain program's by a relative error of at most 0.009.
Values may be sent and summed in bfloat16 or wider, within the bound.
No kernel may reach another device: no remote copies, remote signals or barrier semaphores. Data moves between devices by JAX's collectives and lax.ppermute only.
A program may use at most 64 MiB of HBM per device.

v0:
```python
import functools

import jax
import jax.numpy as jnp
from jax import lax
from jax.experimental import pallas as pl
from jax.experimental.pallas import tpu as pltpu
from jax.sharding import Mesh, PartitionSpec as P


WIDE = ("yh", "x", "c")
BLK = ("yl", "z")
BF = jnp.bfloat16
F32 = jnp.float32
VMEM = pltpu.VMEM
WHOLE = pl.BlockSpec(memory_space=VMEM)


def device(yh, x, c, yl, z):
    return (((yh * 4 + x) * 2 + c) * 2 + yl) * 8 + z


def plane_device(c, along, across, z):
    x, y = (across, along) if c == 0 else (along, across)
    return device(y // 2, x, c, y % 2, z)


LARGE = [
    [plane_device(c, n, m, z) for m in range(4)]
    for c in range(2)
    for n in range(4)
    for z in range(8)
]
SMALL = [
    [plane_device(c, n, m, z) for n in range(4) for z in range(8)]
    for c in range(2)
    for m in range(4)
]


GATHER = [
    [device(yh, x, 0, yl, z) for yl in range(2) for z in range(8)]
    for yh in range(2)
    for x in range(4)
] + [
    [device(yh, 2 * pair + n, 1, yl, z) for n in range(2) for z in range(8)]
    for yh in range(2)
    for yl in range(2)
    for pair in range(2)
]


def exchanged(chunks, which):
    return lax.all_to_all(chunks, WIDE + BLK, 0, 0, axis_index_groups=which)


STEPS = (1, 3, 2)


def forward(block, step):
    route = [(g[i], g[(i + step) % 4]) for g in LARGE for i in range(4)]
    return lax.ppermute(block, WIDE + BLK, route)


def swapped(block):
    return lax.ppermute(block, "c", [(0, 1), (1, 0)])


def nt(a, b):
    return lax.dot_general(a, b, (((1,), (1,)), ((), ())), preferred_element_type=F32)


def errors_kernel(step, at_ref, f1_ref, f2_ref, w_ref, t_ref, *refs):
    core, x, y = at_ref[0], at_ref[1], at_ref[2]
    rows = jnp.concatenate([f1_ref[...].reshape(256, 768), f2_ref[...].reshape(256, 768)])
    parts = [
        (half, place(half, x, y, step, n), e_ref)
        for half, e_ref in ((core, refs[-2]), (1 - core, refs[-1]))
        for n in range(2)
    ]
    span = [slice(m * 256, (m + 1) * 256) for m in range(4)]
    scores = nt(rows, w_ref[span[0], :])
    for m, labels in enumerate(span):
        following = nt(rows, w_ref[span[m + 1], :]) if m < 3 else None
        raised = 0.5 * jnp.tanh(0.5 * scores) + 0.5
        for n, (half, (yl, part), e_ref) in enumerate(parts):
            t = t_ref[yl, :, half, part, :, labels].reshape(128, 256).astype(F32)
            errors = (raised[n * 128 : (n + 1) * 128] - t).astype(BF)
            e_ref[yl, :, part, :, labels] = errors.reshape(8, 16, 256)
        scores = following


def errors_of(at, step, blocks, weights, targets, before):
    return pl.pallas_call(
        functools.partial(errors_kernel, step),
        in_specs=[pl.BlockSpec(memory_space=pltpu.SMEM)] + [WHOLE] * (4 + len(before)),
        out_specs=[WHOLE] * 2,
        out_shape=[jax.ShapeDtypeStruct((2, 8, 4, 16, 1024), BF)] * 2,
        input_output_aliases={5: 0, 6: 1} if before else {},
        cost_estimate=pl.CostEstimate(
            flops=1024 * 1024 * 768, bytes_accessed=5 << 20, transcendentals=1 << 19
        ),
        compiler_params=pltpu.CompilerParams(vmem_limit_bytes=12 << 20),
        name="errors",
    )(
        at,
        *[block.reshape(2, 8, 16, 768) for block in blocks],
        weights,
        targets.reshape(2, 8, 2, 4, 16, 1024),
        *before,
    )


def turned_kernel(at_ref, w_ref, out_ref, held_ref, sems):
    pieces = [pl.ds(m * 256, 256) for m in range(4)]
    copies = [
        pltpu.make_async_copy(w_ref.at[piece], held_ref.at[piece], sems.at[m])
        for m, piece in enumerate(pieces)
    ]
    for copy in copies:
        copy.start()
    for piece, copy in zip(pieces, copies):
        copy.wait()
        columns = held_ref[piece, :].T
        for core in range(2):
            mine = jnp.where(at_ref[0] == core, 1, 0)
            for p in range(8):
                first = (2 * p + core) * 48
                out_ref[mine, p * 48 : (p + 1) * 48, piece] = columns[first : first + 48, :]


def turned(at, weights):
    return pl.pallas_call(
        turned_kernel,
        in_specs=[
            pl.BlockSpec(memory_space=pltpu.SMEM),
            pl.BlockSpec(memory_space=pltpu.HBM),
        ],
        out_specs=[WHOLE] * 2,
        out_shape=[
            jax.ShapeDtypeStruct((2, 384, 1024), BF),
            jax.ShapeDtypeStruct((1024, 768), BF),
        ],
        scratch_shapes=[pltpu.SemaphoreType.DMA((4,))],
        cost_estimate=pl.CostEstimate(
            flops=1024 * 1024 * 768, bytes_accessed=5 << 20, transcendentals=0
        ),
        compiler_params=pltpu.CompilerParams(vmem_limit_bytes=8 << 20),
        name="turned",
    )(at, weights)


def theirs_kernel(wt_ref, e_ref, out_ref):
    for g in range(2):
        out_ref[g] = nt(wt_ref[0], e_ref[g * 512 : (g + 1) * 512, :]).astype(BF)


def theirs_of(wt, errors):
    return pl.pallas_call(
        theirs_kernel,
        in_specs=[WHOLE] * 2,
        out_specs=WHOLE,
        out_shape=jax.ShapeDtypeStruct((2, 384, 512), BF),
        cost_estimate=pl.CostEstimate(
            flops=1024 * 1024 * 768, bytes_accessed=4 << 20, transcendentals=0
        ),
        compiler_params=pltpu.CompilerParams(vmem_limit_bytes=8 << 20),
        name="theirs",
    )(wt, errors)


def mine_kernel(wt_ref, e1_ref, e2_ref, out_ref):
    for n, e_ref in enumerate((e1_ref, e2_ref)):
        for g in range(2):
            out_ref[n, g] = nt(wt_ref[1], e_ref[g * 512 : (g + 1) * 512, :])


def mine_of(wt, errors1, errors2):
    whole = pl.BlockSpec(memory_space=VMEM)
    return pl.pallas_call(
        mine_kernel,
        in_specs=[whole] * 3,
        out_specs=whole,
        out_shape=jax.ShapeDtypeStruct((2, 2, 384, 512), F32),
        cost_estimate=pl.CostEstimate(
            flops=2 * 1024 * 1024 * 768, bytes_accessed=8 << 20, transcendentals=0
        ),
        compiler_params=pltpu.CompilerParams(vmem_limit_bytes=8 << 20),
        name="mine",
    )(wt, errors1, errors2)


def join_kernel(at_ref, m_ref, g1_ref, g2_ref, *out_refs):
    core, x, y = at_ref[0], at_ref[1], at_ref[2]
    for step, out_ref in zip((0,) + STEPS, out_refs):
        for r in range(4):
            to_x = jnp.where(core == 0, (x + step) % 4, r)
            to_y = jnp.where(core == 0, r, (y + step) % 4)
            p, yl = (to_y // 2) * 4 + to_x, to_y % 2
            for n, g_ref in enumerate((g2_ref, g1_ref)):
                out_ref[r, :, n * 512 : (n + 1) * 512] = (
                    m_ref[n, yl, p] + g_ref[yl, p].astype(F32)
                ).astype(BF)


def join(at, mine, got1, got2):
    return pl.pallas_call(
        join_kernel,
        in_specs=[pl.BlockSpec(memory_space=pltpu.SMEM)] + [WHOLE] * 3,
        out_specs=[WHOLE] * 4,
        out_shape=[jax.ShapeDtypeStruct((4, 48, 1024), BF)] * 4,
        cost_estimate=pl.CostEstimate(flops=1 << 20, bytes_accessed=6 << 20, transcendentals=0),
        compiler_params=pltpu.CompilerParams(vmem_limit_bytes=8 << 20),
        name="join",
    )(
        at,
        mine.reshape(2, 2, 8, 48, 512),
        got1.reshape(2, 8, 48, 512),
        got2.reshape(2, 8, 48, 512),
    )


def large_kernel(*refs):
    out_ref = refs[4]
    for r in range(4):
        s = refs[0][r].astype(F32)
        for ref in refs[1:4]:
            s = s + ref[r].astype(F32)
        s = s.astype(BF)
        for z in range(8):
            out_ref[r * 8 + z] = jnp.concatenate(
                [s[:, z * 64 : (z + 1) * 64], s[:, 512 + z * 64 : 512 + (z + 1) * 64]], axis=1
            )


def large_total(*blocks):
    return pl.pallas_call(
        large_kernel,
        in_specs=[WHOLE] * 4,
        out_specs=WHOLE,
        out_shape=jax.ShapeDtypeStruct((32, 48, 128), BF),
        cost_estimate=pl.CostEstimate(flops=1 << 20, bytes_accessed=2 << 20, transcendentals=0),
        compiler_params=pltpu.CompilerParams(vmem_limit_bytes=8 << 20),
        name="large_total",
    )(*blocks)


def update_kernel(e1_ref, e2_ref, f1_ref, f2_ref, w_ref, m_ref, nw_ref, nm_ref):
    dims = (((0,), (0,)), ((), ()))
    grad = lax.dot_general(e1_ref[...], f1_ref[...], dims, preferred_element_type=F32)
    grad = grad + lax.dot_general(e2_ref[...], f2_ref[...], dims, preferred_element_type=F32)
    momentum = (0.9 * m_ref[...].astype(F32) + grad).astype(BF)
    nm_ref[...] = momentum
    nw_ref[...] = (w_ref[...].astype(F32) - 0.002 * momentum.astype(F32)).astype(BF)


def update(*operands):
    labels = pl.BlockSpec((256, 768), lambda n: (n, 0))
    columns = pl.BlockSpec((1024, 256), lambda n: (0, n))
    return pl.pallas_call(
        update_kernel,
        grid=(4,),
        in_specs=[columns, columns, WHOLE, WHOLE, labels, labels],
        out_specs=[labels, labels],
        out_shape=[jax.ShapeDtypeStruct((1024, 768), BF)] * 2,
        cost_estimate=pl.CostEstimate(
            flops=4 * 1024 * 1024 * 768, bytes_accessed=12 << 20, transcendentals=0
        ),
        compiler_params=pltpu.CompilerParams(vmem_limit_bytes=24 << 20),
        name="update",
    )(*operands)


def place(core, x, y, step, n):
    from_x, from_y = (x - step) % 4, (y - step) % 4
    return (
        jnp.where(core == 0, n, from_y % 2),
        jnp.where(core == 0, from_x, (from_y // 2) * 2 + n),
    )


def by_block_kernel(at_ref, *refs):
    out_ref = refs[4]
    for step, in_ref in zip((0,) + STEPS, refs):
        for n in range(2):
            yl, part = place(at_ref[0], at_ref[1], at_ref[2], step, n)
            out_ref[yl, :, part] = in_ref[n]


def by_block(at, blocks):
    out = pl.pallas_call(
        by_block_kernel,
        in_specs=[pl.BlockSpec(memory_space=pltpu.SMEM)] + [WHOLE] * 4,
        out_specs=WHOLE,
        out_shape=jax.ShapeDtypeStruct((2, 8, 4, 16, 768), BF),
        cost_estimate=pl.CostEstimate(flops=1 << 20, bytes_accessed=3 << 20, transcendentals=0),
        compiler_params=pltpu.CompilerParams(vmem_limit_bytes=8 << 20),
        name="by_block",
    )(at, *[block.reshape(2, 8, 16, 768) for block in blocks])
    return out.reshape(1024, 768)


def program(features, weights, momentum, targets):
    ic = lax.axis_index("c")
    ix, iyh, iyl = lax.axis_index("x"), lax.axis_index("yh"), lax.axis_index("yl")
    at = jnp.stack([ic, ix, iyh * 2 + iyl]).astype(jnp.int32)
    quarter = jnp.where(ic == 0, ix, iyh * 2 + ix % 2)
    piece = lax.dynamic_slice_in_dim(features, ic * 64 + quarter * 16, 16, 0)
    other = jnp.stack([1 - ic, ix, iyh * 2 + iyl]).astype(jnp.int32)
    piece, at, other = lax.optimization_barrier((piece, at, other))
    a = exchanged(jnp.broadcast_to(piece[None], (16, 16, 768)), GATHER)
    a, weights = lax.optimization_barrier((a, weights))
    a = a.reshape(256, 768)
    blocks = [a] + [forward(a, d) for d in STEPS]
    wt, held = turned(at, weights)
    errors, others = (), []
    for step, block in zip((0,) + STEPS, blocks):
        if step == 1:
            block, errors, wt = lax.optimization_barrier((block, errors, wt))
        others.append(swapped(block))
        errors = errors_of(at, step, (block, others[-1]), held, targets, errors)
    errors1, errors2 = (e.reshape(1024, 1024) for e in errors)
    got1 = swapped(theirs_of(wt, errors1))
    got2 = swapped(theirs_of(wt, errors2))
    own, *chunks = join(at, mine_of(wt, errors1, errors2), got1, got2)
    got = [forward(chunk, d) for chunk, d in zip(chunks, STEPS)]
    rows1, rows2 = by_block(at, blocks), by_block(other, others)
    updated = update(errors1, errors2, rows1, rows2, held, momentum)
    got, updated = lax.optimization_barrier((got, updated))
    new_weights, new_momentum = updated
    u = exchanged(large_total(own, *got), SMALL)
    total = jnp.sum(u.astype(F32), 0).T.astype(BF)
    feature_grad = jnp.where(ic == 0, total, jnp.roll(total, 64, 0))
    return (new_weights, new_momentum, feature_grad)


def solution(mesh):
    fine = Mesh(mesh.devices.reshape(2, 4, 2, 2, 8), WIDE + BLK)
    both = WIDE + BLK
    return jax.shard_map(
        program,
        mesh=fine,
        in_specs=(P(BLK, None), P(both, None), P(both, None), P(None, both)),
        out_specs=(P(both, None), P(both, None), P(BLK, WIDE)),
        check_vma=False,
    )
```

profile of v0, /device:TPU:2, one launch (start us, length us, event | category | flops | bytes accessed | tf_op | source)
XLA Modules:
  0.0 85.4 jit_solution(14273115368153580737)
XLA Ops:
  0.6 0.0 copy-start
  0.7 0.9 %copy-done = bf16[128,768]{1,0:T(8,128)(2,1)S(1)} copy-done((bf16[128,768]{1,0:T(8,128)(2,1)S(1)}, bf16[128,768]{1,0:T(8,128)(2,1)}, u32[]{:S(2)}) %copy-start) | copy-done | bytes 196632
  1.6 0.1 add_add_fusion
  1.7 22.3 %all_to_all.10 = bf16[16,16,768]{2,1,0:T(8,128)(2,1)S(1)} all-to-all(bf16[16,16,768]{2,1,0:T(8,128)(2,1)S(1)} %broadcast_in_dim.2), channel_id=1, replica_groups={{0,1,2,3,4,5,6,7,8,9,10,11,12,13,14,15},{32,33,34,35,36,37,38,39,40,41,..., dimensions={0} | all-to-all | bytes 786432 | tf_op jit(solution)/shard_map/all_to_all | solution.py:54
  23.9 0.0 collective-permute-start.1
  23.9 1.2 %collective-permute-start = (bf16[256,768]{1,0:T(8,128)(2,1)S(1)}, bf16[256,768]{1,0:T(8,128)(2,1)S(1)}, u32[]{:S(2)}, u32[]{:S(2)}) collective-permute-start(bf16[256,768]{1,0:T(8,128)(2,1)S(1)} %bitcast.36), channel_id=1, source_target_pairs={{0,32},{32,64},{64,96},{96,0},{1,33},{33,65},{65,97},{97,1},{2,34}... | collective-permute-start | bytes 1179656 | tf_op jit(solution)/shard_map/ppermute | solution.py:62
  25.1 0.9 %collective-permute-start.4 = (bf16[256,768]{1,0:T(8,128)(2,1)S(1)}, bf16[256,768]{1,0:T(8,128)(2,1)S(1)}, u32[]{:S(2)}, u32[]{:S(2)}) collective-permute-start(bf16[256,768]{1,0:T(8,128)(2,1)S(1)} %bitcast.37), channel_id=1, source_target_pairs={{0,96},{32,0},{64,32},{96,64},{1,97},{33,1},{65,33},{97,65},{2,98}... | collective-permute-start | bytes 1179656 | tf_op jit(solution)/shard_map/ppermute | solution.py:62
  26.0 2.1 %collective-permute-start.2 = (bf16[256,768]{1,0:T(8,128)(2,1)S(1)}, bf16[256,768]{1,0:T(8,128)(2,1)S(1)}, u32[]{:S(2)}, u32[]{:S(2)}) collective-permute-start(bf16[256,768]{1,0:T(8,128)(2,1)S(1)} %bitcast.38), channel_id=1, source_target_pairs={{0,64},{32,96},{64,0},{96,32},{1,65},{33,97},{65,1},{97,33},{2,66}... | collective-permute-start | bytes 1179656 | tf_op jit(solution)/shard_map/ppermute | solution.py:62
  28.1 1.4 %copy-done.2 = bf16[1024,768]{1,0:T(8,128)(2,1)S(1)} copy-done((bf16[1024,768]{1,0:T(8,128)(2,1)S(1)}, bf16[1024,768]{1,0:T(8,128)(2,1)}, u32[]{:S(2)}) %copy-start.2) | copy-done | bytes 1572888
  29.5 2.0 %turned.1 = (bf16[2,384,1024]{2,1,0:T(8,128)(2,1)S(1)}, bf16[1024,768]{1,0:T(8,128)(2,1)S(1)}) custom-call(s32[3]{0:T(128)S(1)} %get-tuple-element.33.at_ref, bf16[1024,768]{1,0:T(8,128)(2,1)S(1)} %copy-done.2), custom_call_target="tpu_custom_call" | custom-call | flops 805306368 | bytes 5242880 | tf_op jit(solution)/shard_map/turned/pallas_call | solution.py:133
  31.5 0.0 collective-permute-done.1
  31.5 1.7 %errors.4 = (bf16[2,8,4,16,1024]{4,3,2,1,0:T(8,128)(2,1)S(1)}, bf16[2,8,4,16,1024]{4,3,2,1,0:T(8,128)(2,1)S(1)}) custom-call(s32[3]{0:T(128)S(1)} %get-tuple-element.33.at_ref, bf16[2,8,16,768]{3,2,1,0:T(8,128)(2,1)S(1)} %bitcast.39, bf16[2,8,16,768]{3,2,1,0:T(8,128)(2,1)S(1)} %bitcast.55, bf16[1024,768]{1,0:T(8,128)(2,1)S(1)} %get-tuple-element.37.w_ref, ...), custom_call_target="tpu_custom_call" | custom-call | flops 805306368 | bytes 5242880 | tf_op jit(solution)/shard_map/errors/pallas_call | solution.py:94
  33.3 0.0 collective-permute-done
  33.3 0.6 collective-permute-start.6
  33.8 0.0 collective-permute-done.4
  33.9 2.2 %collective-permute-start.5 = (bf16[256,768]{1,0:T(8,128)(2,1)S(1)}, bf16[256,768]{1,0:T(8,128)(2,1)S(1)}, u32[]{:S(2)}, u32[]{:S(2)}) collective-permute-start(bf16[256,768]{1,0:T(8,128)(2,1)S(1)} %collective-permute-done.4), channel_id=1, source_target_pairs={{0,16},{16,0},{1,17},{17,1},{2,18},{18,2},{3,19},{19,3},{4,20},{20... | collective-permute-start | bytes 1179656 | tf_op jit(solution)/shard_map/ppermute | solution.py:66
  36.1 2.0 %collective-permute-done.2 = bf16[256,768]{1,0:T(8,128)(2,1)S(1)} collective-permute-done((bf16[256,768]{1,0:T(8,128)(2,1)S(1)}, bf16[256,768]{1,0:T(8,128)(2,1)S(1)}, u32[]{:S(2)}, u32[]{:S(2)}) %collective-permute-start.2) | collective-permute-done | bytes 393248 | tf_op jit(solution)/shard_map/ppermute | solution.py:62
  38.1 0.0 collective-permute-start.3
  38.1 0.0 collective-permute-done.6
  38.1 1.7 %errors.5 = (bf16[2,8,4,16,1024]{4,3,2,1,0:T(8,128)(2,1)S(1)}, bf16[2,8,4,16,1024]{4,3,2,1,0:T(8,128)(2,1)S(1)}) custom-call(s32[3]{0:T(128)S(1)} %get-tuple-element.33.at_ref, bf16[2,8,16,768]{3,2,1,0:T(8,128)(2,1)S(1)} %bitcast.41, bf16[2,8,16,768]{3,2,1,0:T(8,128)(2,1)S(1)} %bitcast.47, ...), custom_call_target="tpu_custom_call", output_to_operand_aliasing={{0}: (5, {}), {1}: (6, {})} | custom-call | flops 805306368 | bytes 5242880 | tf_op jit(solution)/shard_map/errors/pallas_call | solution.py:94
  39.8 0.0 collective-permute-done.5
  39.8 1.7 %errors.6 = (bf16[2,8,4,16,1024]{4,3,2,1,0:T(8,128)(2,1)S(1)}, bf16[2,8,4,16,1024]{4,3,2,1,0:T(8,128)(2,1)S(1)}) custom-call(s32[3]{0:T(128)S(1)} %get-tuple-element.33.at_ref, bf16[2,8,16,768]{3,2,1,0:T(8,128)(2,1)S(1)} %bitcast.43, bf16[2,8,16,768]{3,2,1,0:T(8,128)(2,1)S(1)} %bitcast.49, ...), custom_call_target="tpu_custom_call", output_to_operand_aliasing={{0}: (5, {}), {1}: (6, {})} | custom-call | flops 805306368 | bytes 5242880 | tf_op jit(solution)/shard_map/errors/pallas_call | solution.py:94
  41.5 0.0 collective-permute-done.3
  41.6 1.7 %errors.7 = (bf16[2,8,4,16,1024]{4,3,2,1,0:T(8,128)(2,1)S(1)}, bf16[2,8,4,16,1024]{4,3,2,1,0:T(8,128)(2,1)S(1)}) custom-call(s32[3]{0:T(128)S(1)} %get-tuple-element.33.at_ref, bf16[2,8,16,768]{3,2,1,0:T(8,128)(2,1)S(1)} %bitcast.45, bf16[2,8,16,768]{3,2,1,0:T(8,128)(2,1)S(1)} %bitcast.51, ...), custom_call_target="tpu_custom_call", output_to_operand_aliasing={{0}: (5, {}), {1}: (6, {})} | custom-call | flops 805306368 | bytes 5242880 | tf_op jit(solution)/shard_map/errors/pallas_call | solution.py:94
  43.3 1.0 %theirs.3 = bf16[2,384,512]{2,1,0:T(8,128)(2,1)S(1)} custom-call(bf16[2,384,1024]{2,1,0:T(8,128)(2,1)S(1)} %get-tuple-element.41.wt_ref, bf16[1024,1024]{1,0:T(8,128)(2,1)S(1)} %bitcast.31), custom_call_target="tpu_custom_call" | custom-call | flops 805306368 | bytes 4194304 | tf_op jit(solution)/shard_map/theirs/pallas_call | solution.py:159
  44.3 0.6 collective-permute-start.8
  44.9 1.0 %theirs.2 = bf16[2,384,512]{2,1,0:T(8,128)(2,1)S(1)} custom-call(bf16[2,384,1024]{2,1,0:T(8,128)(2,1)S(1)} %get-tuple-element.41.wt_ref, bf16[1024,1024]{1,0:T(8,128)(2,1)S(1)} %bitcast.28), custom_call_target="tpu_custom_call" | custom-call | flops 805306368 | bytes 4194304 | tf_op jit(solution)/shard_map/theirs/pallas_call | solution.py:159
  45.9 0.3 collective-permute-start.7
  46.2 1.8 %mine.1 = f32[2,2,384,512]{3,2,1,0:T(8,128)S(1)} custom-call(bf16[2,384,1024]{2,1,0:T(8,128)(2,1)S(1)} %get-tuple-element.41.wt_ref, bf16[1024,1024]{1,0:T(8,128)(2,1)S(1)} %bitcast.29, bf16[1024,1024]{1,0:T(8,128)(2,1)S(1)} %bitcast.32), custom_call_target="tpu_custom_call" | custom-call | flops 1610612736 | bytes 8388608 | tf_op jit(solution)/shard_map/mine/pallas_call | solution.py:180
  48.0 0.0 collective-permute-done.8
  48.1 0.4 collective-permute-done.7
  48.5 0.8 join.1
  49.3 0.7 collective-permute-start.10
  50.0 1.2 %collective-permute-start.11 = (bf16[4,48,1024]{2,1,0:T(8,128)(2,1)S(1)}, bf16[4,48,1024]{2,1,0:T(8,128)(2,1)S(1)}, u32[]{:S(2)}, u32[]{:S(2)}) collective-permute-start(bf16[4,48,1024]{2,1,0:T(8,128)(2,1)S(1)} %get-tuple-element.53), channel_id=1, source_target_pairs={{0,64},{32,96},{64,0},{96,32},{1,65},{33,97},{65,1},{97,33},{2,66}... | collective-permute-start | bytes 1179656 | tf_op jit(solution)/shard_map/ppermute | solution.py:62
  51.2 2.5 %collective-permute-start.9 = (bf16[4,48,1024]{2,1,0:T(8,128)(2,1)S(1)}, bf16[4,48,1024]{2,1,0:T(8,128)(2,1)S(1)}, u32[]{:S(2)}, u32[]{:S(2)}) collective-permute-start(bf16[4,48,1024]{2,1,0:T(8,128)(2,1)S(1)} %get-tuple-element.51), channel_id=1, source_target_pairs={{0,32},{32,64},{64,96},{96,0},{1,33},{33,65},{65,97},{97,1},{2,34}... | collective-permute-start | bytes 1179656 | tf_op jit(solution)/shard_map/ppermute | solution.py:62
  53.7 0.7 by_block.2
  54.4 0.0 copy-start.3
  54.4 0.7 by_block.3
  55.1 0.7 copy-done.3
  55.8 5.8 %update.1 = (bf16[1024,768]{1,0:T(8,128)(2,1)}, bf16[1024,768]{1,0:T(8,128)(2,1)}) custom-call(bf16[1024,1024]{1,0:T(8,128)(2,1)S(1)} %bitcast.30, bf16[1024,1024]{1,0:T(8,128)(2,1)S(1)} %bitcast.33, bf16[1024,768]{1,0:T(8,128)(2,1)S(1)} %bitcast.53, bf16[1024,768]{1,0:T(8,128)(2,1)S(1)} %bitcast.54, bf16[1024,768]{1,0:T(8,128)(2,1)S(1)} %get-tuple-element.37.w_ref, ...), custom_call_target="tpu_custom_call" | custom-call | flops 3221225472 | bytes 12582912 | tf_op jit(solution)/shard_map/update/pallas_call | solution.py:260
  61.7 0.0 collective-permute-done.10.refs_2_
  61.7 0.0 collective-permute-done.11.refs_3_
  61.7 1.8 %collective-permute-done.9.refs_1_ = bf16[4,48,1024]{2,1,0:T(8,128)(2,1)S(1)} collective-permute-done((bf16[4,48,1024]{2,1,0:T(8,128)(2,1)S(1)}, bf16[4,48,1024]{2,1,0:T(8,128)(2,1)S(1)}, u32[]{:S(2)}, u32[]{:S(2)}) %collective-permute-start.9) | collective-permute-done | bytes 393248 | tf_op jit(solution)/shard_map/ppermute | solution.py:62
  63.5 0.3 large_total.1
  63.8 20.8 %all_to_all.11 = bf16[32,48,128]{2,1,0:T(8,128)(2,1)S(1)} all-to-all(bf16[32,48,128]{2,1,0:T(8,128)(2,1)S(1)} %large_total.1), channel_id=1, replica_groups={{0,1,2,3,4,5,6,7,8,9,10,11,12,13,14,15,128,129,130,131,132,133,134,135,..., dimensions={0} | all-to-all | bytes 786432 | tf_op jit(solution)/shard_map/all_to_all | solution.py:54
  84.6 0.1 reduce_sum.12
  84.6 0.1 fusion
  84.7 0.7 maximum_select_fusion
  (5 shorter events, 0.0 us)
Async XLA Ops:
  0.6 0.9 %copy-start = (bf16[128,768]{1,0:T(8,128)(2,1)S(1)}, bf16[128,768]{1,0:T(8,128)(2,1)}, u32[]{:S(2)}) copy-start(bf16[128,768]{1,0:T(8,128)(2,1)} %param.4) | copy-start | bytes 589828
  1.6 29.9 %copy-start.1 = (bf16[2048,1024]{1,0:T(8,128)(2,1)S(1)}, bf16[2048,1024]{1,0:T(8,128)(2,1)}, u32[]{:S(2)}) copy-start(bf16[2048,1024]{1,0:T(8,128)(2,1)} %param.7) | copy-start | bytes 12582916
  23.9 7.6 %collective-permute-start.1 = (bf16[256,768]{1,0:T(8,128)(2,1)S(1)}, bf16[256,768]{1,0:T(8,128)(2,1)S(1)}, u32[]{:S(2)}, u32[]{:S(2)}) collective-permute-start(bf16[256,768]{1,0:T(8,128)(2,1)S(1)} %bitcast.35), channel_id=1, source_target_pairs={{0,16},{16,0},{1,17},{17,1},{2,18},{18,2},{3,19},{19,3},{4,20},{20... | collective-permute-start | bytes 1179656 | tf_op jit(solution)/shard_map/ppermute | solution.py:66
  23.9 9.3 %collective-permute-start = (bf16[256,768]{1,0:T(8,128)(2,1)S(1)}, bf16[256,768]{1,0:T(8,128)(2,1)S(1)}, u32[]{:S(2)}, u32[]{:S(2)}) collective-permute-start(bf16[256,768]{1,0:T(8,128)(2,1)S(1)} %bitcast.36), channel_id=1, source_target_pairs={{0,32},{32,64},{64,96},{96,0},{1,33},{33,65},{65,97},{97,1},{2,34}... | collective-permute-start | bytes 1179656 | tf_op jit(solution)/shard_map/ppermute | solution.py:62
  25.1 8.7 %collective-permute-start.4 = (bf16[256,768]{1,0:T(8,128)(2,1)S(1)}, bf16[256,768]{1,0:T(8,128)(2,1)S(1)}, u32[]{:S(2)}, u32[]{:S(2)}) collective-permute-start(bf16[256,768]{1,0:T(8,128)(2,1)S(1)} %bitcast.37), channel_id=1, source_target_pairs={{0,96},{32,0},{64,32},{96,64},{1,97},{33,1},{65,33},{97,65},{2,98}... | collective-permute-start | bytes 1179656 | tf_op jit(solution)/shard_map/ppermute | solution.py:62
  26.0 12.1 %collective-permute-start.2 = (bf16[256,768]{1,0:T(8,128)(2,1)S(1)}, bf16[256,768]{1,0:T(8,128)(2,1)S(1)}, u32[]{:S(2)}, u32[]{:S(2)}) collective-permute-start(bf16[256,768]{1,0:T(8,128)(2,1)S(1)} %bitcast.38), channel_id=1, source_target_pairs={{0,64},{32,96},{64,0},{96,32},{1,65},{33,97},{65,1},{97,33},{2,66}... | collective-permute-start | bytes 1179656 | tf_op jit(solution)/shard_map/ppermute | solution.py:62
  28.1 1.4 %copy-start.2 = (bf16[1024,768]{1,0:T(8,128)(2,1)S(1)}, bf16[1024,768]{1,0:T(8,128)(2,1)}, u32[]{:S(2)}) copy-start(bf16[1024,768]{1,0:T(8,128)(2,1)} %w_ref) | copy-start | bytes 4718596
  33.3 4.8 %collective-permute-start.6 = (bf16[256,768]{1,0:T(8,128)(2,1)S(1)}, bf16[256,768]{1,0:T(8,128)(2,1)S(1)}, u32[]{:S(2)}, u32[]{:S(2)}) collective-permute-start(bf16[256,768]{1,0:T(8,128)(2,1)S(1)} %collective-permute-done), channel_id=1, source_target_pairs={{0,16},{16,0},{1,17},{17,1},{2,18},{18,2},{3,19},{19,3},{4,20},{20... | collective-permute-start | bytes 1179656 | tf_op jit(solution)/shard_map/ppermute | solution.py:66
  33.9 5.9 %collective-permute-start.5 = (bf16[256,768]{1,0:T(8,128)(2,1)S(1)}, bf16[256,768]{1,0:T(8,128)(2,1)S(1)}, u32[]{:S(2)}, u32[]{:S(2)}) collective-permute-start(bf16[256,768]{1,0:T(8,128)(2,1)S(1)} %collective-permute-done.4), channel_id=1, source_target_pairs={{0,16},{16,0},{1,17},{17,1},{2,18},{18,2},{3,19},{19,3},{4,20},{20... | collective-permute-start | bytes 1179656 | tf_op jit(solution)/shard_map/ppermute | solution.py:66
  38.1 3.5 %collective-permute-start.3 = (bf16[256,768]{1,0:T(8,128)(2,1)S(1)}, bf16[256,768]{1,0:T(8,128)(2,1)S(1)}, u32[]{:S(2)}, u32[]{:S(2)}) collective-permute-start(bf16[256,768]{1,0:T(8,128)(2,1)S(1)} %collective-permute-done.2), channel_id=1, source_target_pairs={{0,16},{16,0},{1,17},{17,1},{2,18},{18,2},{3,19},{19,3},{4,20},{20... | collective-permute-start | bytes 1179656 | tf_op jit(solution)/shard_map/ppermute | solution.py:66
  44.3 3.7 %collective-permute-start.8 = (bf16[2,384,512]{2,1,0:T(8,128)(2,1)S(1)}, bf16[2,384,512]{2,1,0:T(8,128)(2,1)S(1)}, u32[]{:S(2)}, u32[]{:S(2)}) collective-permute-start(bf16[2,384,512]{2,1,0:T(8,128)(2,1)S(1)} %theirs.3), channel_id=1, source_target_pairs={{0,16},{16,0},{1,17},{17,1},{2,18},{18,2},{3,19},{19,3},{4,20},{20... | collective-permute-start | bytes 2359304 | tf_op jit(solution)/shard_map/ppermute | solution.py:66
  45.9 2.6 %collective-permute-start.7 = (bf16[2,384,512]{2,1,0:T(8,128)(2,1)S(1)}, bf16[2,384,512]{2,1,0:T(8,128)(2,1)S(1)}, u32[]{:S(2)}, u32[]{:S(2)}) collective-permute-start(bf16[2,384,512]{2,1,0:T(8,128)(2,1)S(1)} %theirs.2), channel_id=1, source_target_pairs={{0,16},{16,0},{1,17},{17,1},{2,18},{18,2},{3,19},{19,3},{4,20},{20... | collective-permute-start | bytes 2359304 | tf_op jit(solution)/shard_map/ppermute | solution.py:66
  49.3 12.3 %collective-permute-start.10 = (bf16[4,48,1024]{2,1,0:T(8,128)(2,1)S(1)}, bf16[4,48,1024]{2,1,0:T(8,128)(2,1)S(1)}, u32[]{:S(2)}, u32[]{:S(2)}) collective-permute-start(bf16[4,48,1024]{2,1,0:T(8,128)(2,1)S(1)} %get-tuple-element.52), channel_id=1, source_target_pairs={{0,96},{32,0},{64,32},{96,64},{1,97},{33,1},{65,33},{97,65},{2,98}... | collective-permute-start | bytes 1179656 | tf_op jit(solution)/shard_map/ppermute | solution.py:62
  50.0 11.7 %collective-permute-start.11 = (bf16[4,48,1024]{2,1,0:T(8,128)(2,1)S(1)}, bf16[4,48,1024]{2,1,0:T(8,128)(2,1)S(1)}, u32[]{:S(2)}, u32[]{:S(2)}) collective-permute-start(bf16[4,48,1024]{2,1,0:T(8,128)(2,1)S(1)} %get-tuple-element.53), channel_id=1, source_target_pairs={{0,64},{32,96},{64,0},{96,32},{1,65},{33,97},{65,1},{97,33},{2,66}... | collective-permute-start | bytes 1179656 | tf_op jit(solution)/shard_map/ppermute | solution.py:62
  51.2 12.3 %collective-permute-start.9 = (bf16[4,48,1024]{2,1,0:T(8,128)(2,1)S(1)}, bf16[4,48,1024]{2,1,0:T(8,128)(2,1)S(1)}, u32[]{:S(2)}, u32[]{:S(2)}) collective-permute-start(bf16[4,48,1024]{2,1,0:T(8,128)(2,1)S(1)} %get-tuple-element.51), channel_id=1, source_target_pairs={{0,32},{32,64},{64,96},{96,0},{1,33},{33,65},{65,97},{97,1},{2,34}... | collective-permute-start | bytes 1179656 | tf_op jit(solution)/shard_map/ppermute | solution.py:62
  54.4 1.4 %copy-start.3 = (bf16[1024,768]{1,0:T(8,128)(2,1)S(1)}, bf16[1024,768]{1,0:T(8,128)(2,1)}, u32[]{:S(2)}) copy-start(bf16[1024,768]{1,0:T(8,128)(2,1)} %m_ref.1) | copy-start | bytes 4718596
where the time goes:
time: 86.2 us; the launch traced here: 85.4 us
  blocking collectives  43.1 us (50%)
  Pallas kernels  21 us (24%)
  starting transfers between devices  12.3 us (14%)
  waiting for transfers between devices  4.28 us (5%)
  local copies, waits for them, and re-layouts  3.12 us (4%)
    all_to_all x2, blocking collectives, exchanged(): return lax.all_to_all(chunks, WIDE + BLK, 0, 0, axis_index_groups=which)  43.1 us
    ppermute x6, starting transfers between devices, forward(): return lax.ppermute(block, WIDE + BLK, route)  8.58 us
    pallas_call x4, Pallas kernels, errors_of(): pl.pallas_call(functools.partial(errors_kernel, step), in_specs=[pl.Block...  6.92 us
    pallas_call x1, Pallas kernels, update(): pl.pallas_call(update_kernel, grid=(4,), in_specs=[columns, columns, WHOL...  5.81 us
    ppermute x6, waiting for transfers between devices, forward(): return lax.ppermute(block, WIDE + BLK, route)  3.83 us
    ppermute x6, starting transfers between devices, swapped(): return lax.ppermute(block, 'c', [(0, 1), (1, 0)])  3.69 us
    unnamed x8, local copies, waits for them, and re-layouts  3.02 us
    pallas_call x2, Pallas kernels, theirs_of(): pl.pallas_call(theirs_kernel, in_specs=[WHOLE] * 2, out_specs=WHOLE, out_...  2.02 us
  transfers between devices with their start and end apart: 12, of which 3 were waited for; matrix products, arithmetic and copies ran while one was open for 0% of the time, Pallas kernels for 20%

commit v1 on v0

--- a/solution.py
+++ b/solution.py
@@ -111,17 +111,12 @@
     )
 
 
-def turned_kernel(at_ref, w_ref, out_ref, held_ref, sems):
-    pieces = [pl.ds(m * 256, 256) for m in range(4)]
-    copies = [
-        pltpu.make_async_copy(w_ref.at[piece], held_ref.at[piece], sems.at[m])
-        for m, piece in enumerate(pieces)
-    ]
-    for copy in copies:
-        copy.start()
-    for piece, copy in zip(pieces, copies):
-        copy.wait()
-        columns = held_ref[piece, :].T
+def turned_kernel(at_ref, w_ref, out_ref, held_ref):
+    for m in range(4):
+        piece = slice(m * 256, (m + 1) * 256)
+        rows = w_ref[piece, :]
+        held_ref[piece, :] = rows
+        columns = rows.T
         for core in range(2):
             mine = jnp.where(at_ref[0] == core, 1, 0)
             for p in range(8):
@@ -132,16 +127,12 @@
 def turned(at, weights):
     return pl.pallas_call(
         turned_kernel,
-        in_specs=[
-            pl.BlockSpec(memory_space=pltpu.SMEM),
-            pl.BlockSpec(memory_space=pltpu.HBM),
-        ],
+        in_specs=[pl.BlockSpec(memory_space=pltpu.SMEM), WHOLE],
         out_specs=[WHOLE] * 2,
         out_shape=[
             jax.ShapeDtypeStruct((2, 384, 1024), BF),
             jax.ShapeDtypeStruct((1024, 768), BF),
         ],
-        scratch_shapes=[pltpu.SemaphoreType.DMA((4,))],
         cost_estimate=pl.CostEstimate(
             flops=1024 * 1024 * 768, bytes_accessed=5 << 20, transcendentals=0
         ),

time: 86.2 us -> 86.2 us (level)
  Pallas kernels: 21 us -> 20.1 us
  starting transfers between devices: 12.3 us -> 13.2 us
    ppermute x6, starting transfers between devices: 3.69 us -> 4.61 us  [swapped(): return lax.ppermute(block, 'c', [(0, 1), (1, 0)])]
    pallas_call x1, Pallas kernels: 1.98 us -> 1.06 us  [turned(): pl.pallas_call(turned_kernel, in_specs=[pl.BlockSpec(memory_space=pltpu.S...]
  transfers between devices with their start and end apart: 12 -> 12, of which waited for: 3 -> 3; matrix products, arithmetic and copies ran while one was open for 0% -> 0% of each run, Pallas kernels for 20% -> 19%
where the time goes in v1:
time: 86.2 us; the launch traced here: 85.4 us
  blocking collectives  43.1 us (50%)
  Pallas kernels  20.1 us (23%)
  starting transfers between devices  13.2 us (15%)
  waiting for transfers between devices  4.28 us (5%)
  local copies, waits for them, and re-layouts  3.12 us (4%)
    all_to_all x2, blocking collectives, exchanged(): return lax.all_to_all(chunks, WIDE + BLK, 0, 0, axis_index_groups=which)  43.1 us
    ppermute x6, starting transfers between devices, forward(): return lax.ppermute(block, WIDE + BLK, route)  8.58 us
    pallas_call x4, Pallas kernels, errors_of(): pl.pallas_call(functools.partial(errors_kernel, step), in_specs=[pl.Block...  6.92 us
    pallas_call x1, Pallas kernels, update(): pl.pallas_call(update_kernel, grid=(4,), in_specs=[columns, columns, WHOL...  5.81 us
    ppermute x6, starting transfers between devices, swapped(): return lax.ppermute(block, 'c', [(0, 1), (1, 0)])  4.61 us
    ppermute x6, waiting for transfers between devices, forward(): return lax.ppermute(block, WIDE + BLK, route)  3.83 us
    unnamed x8, local copies, waits for them, and re-layouts  3.02 us
    pallas_call x2, Pallas kernels, theirs_of(): pl.pallas_call(theirs_kernel, in_specs=[WHOLE] * 2, out_specs=WHOLE, out_...  2.02 us
  transfers between devices with their start and end apart: 12, of which 3 were waited for; matrix products, arithmetic and copies ran while one was open for 0% of the time, Pallas kernels for 19%

profile of v1, /device:TPU:2, one launch (start us, length us, event | category | flops | bytes accessed | tf_op | source)
XLA Modules:
  0.0 85.4 jit_solution(9472856160208660457)
XLA Ops:
  0.6 0.0 copy-start
  0.7 0.9 %copy-done = bf16[128,768]{1,0:T(8,128)(2,1)S(1)} copy-done((bf16[128,768]{1,0:T(8,128)(2,1)S(1)}, bf16[128,768]{1,0:T(8,128)(2,1)}, u32[]{:S(2)}) %copy-start) | copy-done | bytes 196632
  1.6 0.1 add_add_fusion
  1.7 22.3 %all_to_all.10 = bf16[16,16,768]{2,1,0:T(8,128)(2,1)S(1)} all-to-all(bf16[16,16,768]{2,1,0:T(8,128)(2,1)S(1)} %broadcast_in_dim.2), channel_id=1, replica_groups={{0,1,2,3,4,5,6,7,8,9,10,11,12,13,14,15},{32,33,34,35,36,37,38,39,40,41,..., dimensions={0} | all-to-all | bytes 786432 | tf_op jit(solution)/shard_map/all_to_all | solution.py:54
  23.9 0.0 collective-permute-start.1
  23.9 1.2 %collective-permute-start = (bf16[256,768]{1,0:T(8,128)(2,1)S(1)}, bf16[256,768]{1,0:T(8,128)(2,1)S(1)}, u32[]{:S(2)}, u32[]{:S(2)}) collective-permute-start(bf16[256,768]{1,0:T(8,128)(2,1)S(1)} %bitcast.36), channel_id=1, source_target_pairs={{0,32},{32,64},{64,96},{96,0},{1,33},{33,65},{65,97},{97,1},{2,34}... | collective-permute-start | bytes 1179656 | tf_op jit(solution)/shard_map/ppermute | solution.py:62
  25.1 0.9 %collective-permute-start.4 = (bf16[256,768]{1,0:T(8,128)(2,1)S(1)}, bf16[256,768]{1,0:T(8,128)(2,1)S(1)}, u32[]{:S(2)}, u32[]{:S(2)}) collective-permute-start(bf16[256,768]{1,0:T(8,128)(2,1)S(1)} %bitcast.37), channel_id=1, source_target_pairs={{0,96},{32,0},{64,32},{96,64},{1,97},{33,1},{65,33},{97,65},{2,98}... | collective-permute-start | bytes 1179656 | tf_op jit(solution)/shard_map/ppermute | solution.py:62
  26.0 2.1 %collective-permute-start.2 = (bf16[256,768]{1,0:T(8,128)(2,1)S(1)}, bf16[256,768]{1,0:T(8,128)(2,1)S(1)}, u32[]{:S(2)}, u32[]{:S(2)}) collective-permute-start(bf16[256,768]{1,0:T(8,128)(2,1)S(1)} %bitcast.38), channel_id=1, source_target_pairs={{0,64},{32,96},{64,0},{96,32},{1,65},{33,97},{65,1},{97,33},{2,66}... | collective-permute-start | bytes 1179656 | tf_op jit(solution)/shard_map/ppermute | solution.py:62
  28.1 1.4 %copy-done.2 = bf16[1024,768]{1,0:T(8,128)(2,1)S(1)} copy-done((bf16[1024,768]{1,0:T(8,128)(2,1)S(1)}, bf16[1024,768]{1,0:T(8,128)(2,1)}, u32[]{:S(2)}) %copy-start.2) | copy-done | bytes 1572888
  29.5 1.1 %turned.1 = (bf16[2,384,1024]{2,1,0:T(8,128)(2,1)S(1)}, bf16[1024,768]{1,0:T(8,128)(2,1)S(1)}) custom-call(s32[3]{0:T(128)S(1)} %get-tuple-element.33.at_ref, bf16[1024,768]{1,0:T(8,128)(2,1)S(1)} %copy-done.2), custom_call_target="tpu_custom_call" | custom-call | flops 805306368 | bytes 5242880 | tf_op jit(solution)/shard_map/turned/pallas_call | solution.py:128
  30.6 0.0 collective-permute-done.1
  30.6 1.7 %errors.4 = (bf16[2,8,4,16,1024]{4,3,2,1,0:T(8,128)(2,1)S(1)}, bf16[2,8,4,16,1024]{4,3,2,1,0:T(8,128)(2,1)S(1)}) custom-call(s32[3]{0:T(128)S(1)} %get-tuple-element.33.at_ref, bf16[2,8,16,768]{3,2,1,0:T(8,128)(2,1)S(1)} %bitcast.39, bf16[2,8,16,768]{3,2,1,0:T(8,128)(2,1)S(1)} %bitcast.55, bf16[1024,768]{1,0:T(8,128)(2,1)S(1)} %get-tuple-element.37.w_ref, ...), custom_call_target="tpu_custom_call" | custom-call | flops 805306368 | bytes 5242880 | tf_op jit(solution)/shard_map/errors/pallas_call | solution.py:94
  32.3 0.0 collective-permute-done
  32.3 0.6 collective-permute-start.6
  32.9 0.0 collective-permute-done.4
  32.9 3.1 %collective-permute-start.5 = (bf16[256,768]{1,0:T(8,128)(2,1)S(1)}, bf16[256,768]{1,0:T(8,128)(2,1)S(1)}, u32[]{:S(2)}, u32[]{:S(2)}) collective-permute-start(bf16[256,768]{1,0:T(8,128)(2,1)S(1)} %collective-permute-done.4), channel_id=1, source_target_pairs={{0,16},{16,0},{1,17},{17,1},{2,18},{18,2},{3,19},{19,3},{4,20},{20... | collective-permute-start | bytes 1179656 | tf_op jit(solution)/shard_map/ppermute | solution.py:66
  36.1 2.0 %collective-permute-done.2 = bf16[256,768]{1,0:T(8,128)(2,1)S(1)} collective-permute-done((bf16[256,768]{1,0:T(8,128)(2,1)S(1)}, bf16[256,768]{1,0:T(8,128)(2,1)S(1)}, u32[]{:S(2)}, u32[]{:S(2)}) %collective-permute-start.2) | collective-permute-done | bytes 393248 | tf_op jit(solution)/shard_map/ppermute | solution.py:62
  38.1 0.0 collective-permute-start.3
  38.1 0.0 collective-permute-done.6
  38.1 1.7 %errors.5 = (bf16[2,8,4,16,1024]{4,3,2,1,0:T(8,128)(2,1)S(1)}, bf16[2,8,4,16,1024]{4,3,2,1,0:T(8,128)(2,1)S(1)}) custom-call(s32[3]{0:T(128)S(1)} %get-tuple-element.33.at_ref, bf16[2,8,16,768]{3,2,1,0:T(8,128)(2,1)S(1)} %bitcast.41, bf16[2,8,16,768]{3,2,1,0:T(8,128)(2,1)S(1)} %bitcast.47, ...), custom_call_target="tpu_custom_call", output_to_operand_aliasing={{0}: (5, {}), {1}: (6, {})} | custom-call | flops 805306368 | bytes 5242880 | tf_op jit(solution)/shard_map/errors/pallas_call | solution.py:94
  39.8 0.0 collective-permute-done.5
  39.8 1.7 %errors.6 = (bf16[2,8,4,16,1024]{4,3,2,1,0:T(8,128)(2,1)S(1)}, bf16[2,8,4,16,1024]{4,3,2,1,0:T(8,128)(2,1)S(1)}) custom-call(s32[3]{0:T(128)S(1)} %get-tuple-element.33.at_ref, bf16[2,8,16,768]{3,2,1,0:T(8,128)(2,1)S(1)} %bitcast.43, bf16[2,8,16,768]{3,2,1,0:T(8,128)(2,1)S(1)} %bitcast.49, ...), custom_call_target="tpu_custom_call", output_to_operand_aliasing={{0}: (5, {}), {1}: (6, {})} | custom-call | flops 805306368 | bytes 5242880 | tf_op jit(solution)/shard_map/errors/pallas_call | solution.py:94
  41.5 0.0 collective-permute-done.3
  41.6 1.7 %errors.7 = (bf16[2,8,4,16,1024]{4,3,2,1,0:T(8,128)(2,1)S(1)}, bf16[2,8,4,16,1024]{4,3,2,1,0:T(8,128)(2,1)S(1)}) custom-call(s32[3]{0:T(128)S(1)} %get-tuple-element.33.at_ref, bf16[2,8,16,768]{3,2,1,0:T(8,128)(2,1)S(1)} %bitcast.45, bf16[2,8,16,768]{3,2,1,0:T(8,128)(2,1)S(1)} %bitcast.51, ...), custom_call_target="tpu_custom_call", output_to_operand_aliasing={{0}: (5, {}), {1}: (6, {})} | custom-call | flops 805306368 | bytes 5242880 | tf_op jit(solution)/shard_map/errors/pallas_call | solution.py:94
  43.3 1.0 %theirs.3 = bf16[2,384,512]{2,1,0:T(8,128)(2,1)S(1)} custom-call(bf16[2,384,1024]{2,1,0:T(8,128)(2,1)S(1)} %get-tuple-element.41.wt_ref, bf16[1024,1024]{1,0:T(8,128)(2,1)S(1)} %bitcast.31), custom_call_target="tpu_custom_call" | custom-call | flops 805306368 | bytes 4194304 | tf_op jit(solution)/shard_map/theirs/pallas_call | solution.py:150
  44.3 0.6 collective-permute-start.8
  44.9 1.0 %theirs.2 = bf16[2,384,512]{2,1,0:T(8,128)(2,1)S(1)} custom-call(bf16[2,384,1024]{2,1,0:T(8,128)(2,1)S(1)} %get-tuple-element.41.wt_ref, bf16[1024,1024]{1,0:T(8,128)(2,1)S(1)} %bitcast.28), custom_call_target="tpu_custom_call" | custom-call | flops 805306368 | bytes 4194304 | tf_op jit(solution)/shard_map/theirs/pallas_call | solution.py:150
  45.9 0.3 collective-permute-start.7
  46.2 1.8 %mine.1 = f32[2,2,384,512]{3,2,1,0:T(8,128)S(1)} custom-call(bf16[2,384,1024]{2,1,0:T(8,128)(2,1)S(1)} %get-tuple-element.41.wt_ref, bf16[1024,1024]{1,0:T(8,128)(2,1)S(1)} %bitcast.29, bf16[1024,1024]{1,0:T(8,128)(2,1)S(1)} %bitcast.32), custom_call_target="tpu_custom_call" | custom-call | flops 1610612736 | bytes 8388608 | tf_op jit(solution)/shard_map/mine/pallas_call | solution.py:171
  48.0 0.0 collective-permute-done.8
  48.1 0.4 collective-permute-done.7
  48.5 0.8 join.1
  49.3 0.7 collective-permute-start.10
  50.0 1.2 %collective-permute-start.11 = (bf16[4,48,1024]{2,1,0:T(8,128)(2,1)S(1)}, bf16[4,48,1024]{2,1,0:T(8,128)(2,1)S(1)}, u32[]{:S(2)}, u32[]{:S(2)}) collective-permute-start(bf16[4,48,1024]{2,1,0:T(8,128)(2,1)S(1)} %get-tuple-element.53), channel_id=1, source_target_pairs={{0,64},{32,96},{64,0},{96,32},{1,65},{33,97},{65,1},{97,33},{2,66}... | collective-permute-start | bytes 1179656 | tf_op jit(solution)/shard_map/ppermute | solution.py:62
  51.2 2.5 %collective-permute-start.9 = (bf16[4,48,1024]{2,1,0:T(8,128)(2,1)S(1)}, bf16[4,48,1024]{2,1,0:T(8,128)(2,1)S(1)}, u32[]{:S(2)}, u32[]{:S(2)}) collective-permute-start(bf16[4,48,1024]{2,1,0:T(8,128)(2,1)S(1)} %get-tuple-element.51), channel_id=1, source_target_pairs={{0,32},{32,64},{64,96},{96,0},{1,33},{33,65},{65,97},{97,1},{2,34}... | collective-permute-start | bytes 1179656 | tf_op jit(solution)/shard_map/ppermute | solution.py:62
  53.7 0.7 by_block.2
  54.4 0.0 copy-start.3
  54.4 0.7 by_block.3
  55.1 0.7 copy-done.3
  55.8 5.8 %update.1 = (bf16[1024,768]{1,0:T(8,128)(2,1)}, bf16[1024,768]{1,0:T(8,128)(2,1)}) custom-call(bf16[1024,1024]{1,0:T(8,128)(2,1)S(1)} %bitcast.30, bf16[1024,1024]{1,0:T(8,128)(2,1)S(1)} %bitcast.33, bf16[1024,768]{1,0:T(8,128)(2,1)S(1)} %bitcast.53, bf16[1024,768]{1,0:T(8,128)(2,1)S(1)} %bitcast.54, bf16[1024,768]{1,0:T(8,128)(2,1)S(1)} %get-tuple-element.37.w_ref, ...), custom_call_target="tpu_custom_call" | custom-call | flops 3221225472 | bytes 12582912 | tf_op jit(solution)/shard_map/update/pallas_call | solution.py:251
  61.7 0.0 collective-permute-done.10.refs_2_
  61.7 0.0 collective-permute-done.11.refs_3_
  61.7 1.8 %collective-permute-done.9.refs_1_ = bf16[4,48,1024]{2,1,0:T(8,128)(2,1)S(1)} collective-permute-done((bf16[4,48,1024]{2,1,0:T(8,128)(2,1)S(1)}, bf16[4,48,1024]{2,1,0:T(8,128)(2,1)S(1)}, u32[]{:S(2)}, u32[]{:S(2)}) %collective-permute-start.9) | collective-permute-done | bytes 393248 | tf_op jit(solution)/shard_map/ppermute | solution.py:62
  63.5 0.3 large_total.1
  63.8 20.8 %all_to_all.11 = bf16[32,48,128]{2,1,0:T(8,128)(2,1)S(1)} all-to-all(bf16[32,48,128]{2,1,0:T(8,128)(2,1)S(1)} %large_total.1), channel_id=1, replica_groups={{0,1,2,3,4,5,6,7,8,9,10,11,12,13,14,15,128,129,130,131,132,133,134,135,..., dimensions={0} | all-to-all | bytes 786432 | tf_op jit(solution)/shard_map/all_to_all | solution.py:54
  84.6 0.1 reduce_sum.12
  84.6 0.1 fusion
  84.7 0.7 maximum_select_fusion
  (5 shorter events, 0.0 us)
Async XLA Ops:
  0.6 0.9 %copy-start = (bf16[128,768]{1,0:T(8,128)(2,1)S(1)}, bf16[128,768]{1,0:T(8,128)(2,1)}, u32[]{:S(2)}) copy-start(bf16[128,768]{1,0:T(8,128)(2,1)} %param.4) | copy-start | bytes 589828
  1.6 28.9 %copy-start.1 = (bf16[2048,1024]{1,0:T(8,128)(2,1)S(1)}, bf16[2048,1024]{1,0:T(8,128)(2,1)}, u32[]{:S(2)}) copy-start(bf16[2048,1024]{1,0:T(8,128)(2,1)} %param.7) | copy-start | bytes 12582916
  23.9 6.6 %collective-permute-start.1 = (bf16[256,768]{1,0:T(8,128)(2,1)S(1)}, bf16[256,768]{1,0:T(8,128)(2,1)S(1)}, u32[]{:S(2)}, u32[]{:S(2)}) collective-permute-start(bf16[256,768]{1,0:T(8,128)(2,1)S(1)} %bitcast.35), channel_id=1, source_target_pairs={{0,16},{16,0},{1,17},{17,1},{2,18},{18,2},{3,19},{19,3},{4,20},{20... | collective-permute-start | bytes 1179656 | tf_op jit(solution)/shard_map/ppermute | solution.py:66
  23.9 8.4 %collective-permute-start = (bf16[256,768]{1,0:T(8,128)(2,1)S(1)}, bf16[256,768]{1,0:T(8,128)(2,1)S(1)}, u32[]{:S(2)}, u32[]{:S(2)}) collective-permute-start(bf16[256,768]{1,0:T(8,128)(2,1)S(1)} %bitcast.36), channel_id=1, source_target_pairs={{0,32},{32,64},{64,96},{96,0},{1,33},{33,65},{65,97},{97,1},{2,34}... | collective-permute-start | bytes 1179656 | tf_op jit(solution)/shard_map/ppermute | solution.py:62
  25.1 7.8 %collective-permute-start.4 = (bf16[256,768]{1,0:T(8,128)(2,1)S(1)}, bf16[256,768]{1,0:T(8,128)(2,1)S(1)}, u32[]{:S(2)}, u32[]{:S(2)}) collective-permute-start(bf16[256,768]{1,0:T(8,128)(2,1)S(1)} %bitcast.37), channel_id=1, source_target_pairs={{0,96},{32,0},{64,32},{96,64},{1,97},{33,1},{65,33},{97,65},{2,98}... | collective-permute-start | bytes 1179656 | tf_op jit(solution)/shard_map/ppermute | solution.py:62
  26.0 12.1 %collective-permute-start.2 = (bf16[256,768]{1,0:T(8,128)(2,1)S(1)}, bf16[256,768]{1,0:T(8,128)(2,1)S(1)}, u32[]{:S(2)}, u32[]{:S(2)}) collective-permute-start(bf16[256,768]{1,0:T(8,128)(2,1)S(1)} %bitcast.38), channel_id=1, source_target_pairs={{0,64},{32,96},{64,0},{96,32},{1,65},{33,97},{65,1},{97,33},{2,66}... | collective-permute-start | bytes 1179656 | tf_op jit(solution)/shard_map/ppermute | solution.py:62
  28.1 1.4 %copy-start.2 = (bf16[1024,768]{1,0:T(8,128)(2,1)S(1)}, bf16[1024,768]{1,0:T(8,128)(2,1)}, u32[]{:S(2)}) copy-start(bf16[1024,768]{1,0:T(8,128)(2,1)} %w_ref) | copy-start | bytes 4718596
  32.3 5.7 %collective-permute-start.6 = (bf16[256,768]{1,0:T(8,128)(2,1)S(1)}, bf16[256,768]{1,0:T(8,128)(2,1)S(1)}, u32[]{:S(2)}, u32[]{:S(2)}) collective-permute-start(bf16[256,768]{1,0:T(8,128)(2,1)S(1)} %collective-permute-done), channel_id=1, source_target_pairs={{0,16},{16,0},{1,17},{17,1},{2,18},{18,2},{3,19},{19,3},{4,20},{20... | collective-permute-start | bytes 1179656 | tf_op jit(solution)/shard_map/ppermute | solution.py:66
  32.9 6.9 %collective-permute-start.5 = (bf16[256,768]{1,0:T(8,128)(2,1)S(1)}, bf16[256,768]{1,0:T(8,128)(2,1)S(1)}, u32[]{:S(2)}, u32[]{:S(2)}) collective-permute-start(bf16[256,768]{1,0:T(8,128)(2,1)S(1)} %collective-permute-done.4), channel_id=1, source_target_pairs={{0,16},{16,0},{1,17},{17,1},{2,18},{18,2},{3,19},{19,3},{4,20},{20... | collective-permute-start | bytes 1179656 | tf_op jit(solution)/shard_map/ppermute | solution.py:66
  38.1 3.5 %collective-permute-start.3 = (bf16[256,768]{1,0:T(8,128)(2,1)S(1)}, bf16[256,768]{1,0:T(8,128)(2,1)S(1)}, u32[]{:S(2)}, u32[]{:S(2)}) collective-permute-start(bf16[256,768]{1,0:T(8,128)(2,1)S(1)} %collective-permute-done.2), channel_id=1, source_target_pairs={{0,16},{16,0},{1,17},{17,1},{2,18},{18,2},{3,19},{19,3},{4,20},{20... | collective-permute-start | bytes 1179656 | tf_op jit(solution)/shard_map/ppermute | solution.py:66
  44.3 3.7 %collective-permute-start.8 = (bf16[2,384,512]{2,1,0:T(8,128)(2,1)S(1)}, bf16[2,384,512]{2,1,0:T(8,128)(2,1)S(1)}, u32[]{:S(2)}, u32[]{:S(2)}) collective-permute-start(bf16[2,384,512]{2,1,0:T(8,128)(2,1)S(1)} %theirs.3), channel_id=1, source_target_pairs={{0,16},{16,0},{1,17},{17,1},{2,18},{18,2},{3,19},{19,3},{4,20},{20... | collective-permute-start | bytes 2359304 | tf_op jit(solution)/shard_map/ppermute | solution.py:66
  45.9 2.6 %collective-permute-start.7 = (bf16[2,384,512]{2,1,0:T(8,128)(2,1)S(1)}, bf16[2,384,512]{2,1,0:T(8,128)(2,1)S(1)}, u32[]{:S(2)}, u32[]{:S(2)}) collective-permute-start(bf16[2,384,512]{2,1,0:T(8,128)(2,1)S(1)} %theirs.2), channel_id=1, source_target_pairs={{0,16},{16,0},{1,17},{17,1},{2,18},{18,2},{3,19},{19,3},{4,20},{20... | collective-permute-start | bytes 2359304 | tf_op jit(solution)/shard_map/ppermute | solution.py:66
  49.3 12.3 %collective-permute-start.10 = (bf16[4,48,1024]{2,1,0:T(8,128)(2,1)S(1)}, bf16[4,48,1024]{2,1,0:T(8,128)(2,1)S(1)}, u32[]{:S(2)}, u32[]{:S(2)}) collective-permute-start(bf16[4,48,1024]{2,1,0:T(8,128)(2,1)S(1)} %get-tuple-element.52), channel_id=1, source_target_pairs={{0,96},{32,0},{64,32},{96,64},{1,97},{33,1},{65,33},{97,65},{2,98}... | collective-permute-start | bytes 1179656 | tf_op jit(solution)/shard_map/ppermute | solution.py:62
  50.0 11.7 %collective-permute-start.11 = (bf16[4,48,1024]{2,1,0:T(8,128)(2,1)S(1)}, bf16[4,48,1024]{2,1,0:T(8,128)(2,1)S(1)}, u32[]{:S(2)}, u32[]{:S(2)}) collective-permute-start(bf16[4,48,1024]{2,1,0:T(8,128)(2,1)S(1)} %get-tuple-element.53), channel_id=1, source_target_pairs={{0,64},{32,96},{64,0},{96,32},{1,65},{33,97},{65,1},{97,33},{2,66}... | collective-permute-start | bytes 1179656 | tf_op jit(solution)/shard_map/ppermute | solution.py:62
  51.2 12.3 %collective-permute-start.9 = (bf16[4,48,1024]{2,1,0:T(8,128)(2,1)S(1)}, bf16[4,48,1024]{2,1,0:T(8,128)(2,1)S(1)}, u32[]{:S(2)}, u32[]{:S(2)}) collective-permute-start(bf16[4,48,1024]{2,1,0:T(8,128)(2,1)S(1)} %get-tuple-element.51), channel_id=1, source_target_pairs={{0,32},{32,64},{64,96},{96,0},{1,33},{33,65},{65,97},{97,1},{2,34}... | collective-permute-start | bytes 1179656 | tf_op jit(solution)/shard_map/ppermute | solution.py:62
  54.4 1.4 %copy-start.3 = (bf16[1024,768]{1,0:T(8,128)(2,1)S(1)}, bf16[1024,768]{1,0:T(8,128)(2,1)}, u32[]{:S(2)}) copy-start(bf16[1024,768]{1,0:T(8,128)(2,1)} %m_ref.1) | copy-start | bytes 4718596

commit v2 on v1

--- a/solution.py
+++ b/solution.py
@@ -234,6 +234,26 @@
         compiler_params=pltpu.CompilerParams(vmem_limit_bytes=8 << 20),
         name="large_total",
     )(*blocks)
+
+
+def small_kernel(at_ref, u_ref, out_ref):
+    s = u_ref[0].astype(F32)
+    for n in range(1, 32):
+        s = s + u_ref[n].astype(F32)
+    turned_halves = jnp.concatenate([s[:, 64:], s[:, :64]], axis=1)
+    out_ref[...] = jnp.where(at_ref[0] == 0, s, turned_halves).astype(BF)
+
+
+def small_total(at, u):
+    return pl.pallas_call(
+        small_kernel,
+        in_specs=[pl.BlockSpec(memory_space=pltpu.SMEM), WHOLE],
+        out_specs=WHOLE,
+        out_shape=jax.ShapeDtypeStruct((48, 128), BF),
+        cost_estimate=pl.CostEstimate(flops=1 << 18, bytes_accessed=1 << 19, transcendentals=0),
+        compiler_params=pltpu.CompilerParams(vmem_limit_bytes=4 << 20),
+        name="small_total",
+    )(at, u)
 
 
 def update_kernel(e1_ref, e2_ref, f1_ref, f2_ref, w_ref, m_ref, nw_ref, nm_ref):
@@ -320,8 +340,7 @@
     got, updated = lax.optimization_barrier((got, updated))
     new_weights, new_momentum = updated
     u = exchanged(large_total(own, *got), SMALL)
-    total = jnp.sum(u.astype(F32), 0).T.astype(BF)
-    feature_grad = jnp.where(ic == 0, total, jnp.roll(total, 64, 0))
+    feature_grad = small_total(at, u).T
     return (new_weights, new_momentum, feature_grad)
 
 

time: 86.2 us -> 86.6 us (level)
  Pallas kernels: 20.1 us -> 21.4 us
    pallas_call x0 -> x1, Pallas kernels: none -> 1.27 us  [small_total(): pl.pallas_call(small_kernel, in_specs=[pl.BlockSpec(memory_space=pltpu.SM...]
where the time goes in v2:
time: 86.6 us; the launch traced here: 85.8 us
  blocking collectives  43.1 us (50%)
  Pallas kernels  21.4 us (25%)
  starting transfers between devices  13.2 us (15%)
  waiting for transfers between devices  4.27 us (5%)
  local copies, waits for them, and re-layouts  3.05 us (4%)
    all_to_all x2, blocking collectives, exchanged(): return lax.all_to_all(chunks, WIDE + BLK, 0, 0, axis_index_groups=which)  43.1 us
    ppermute x6, starting transfers between devices, forward(): return lax.ppermute(block, WIDE + BLK, route)  8.58 us
    pallas_call x4, Pallas kernels, errors_of(): pl.pallas_call(functools.partial(errors_kernel, step), in_specs=[pl.Block...  6.92 us
    pallas_call x1, Pallas kernels, update(): pl.pallas_call(update_kernel, grid=(4,), in_specs=[columns, columns, WHOL...  5.81 us
    ppermute x6, starting transfers between devices, swapped(): return lax.ppermute(block, 'c', [(0, 1), (1, 0)])  4.62 us
    ppermute x6, waiting for transfers between devices, forward(): return lax.ppermute(block, WIDE + BLK, route)  3.83 us
    unnamed x8, local copies, waits for them, and re-layouts  3.02 us
    pallas_call x2, Pallas kernels, theirs_of(): pl.pallas_call(theirs_kernel, in_specs=[WHOLE] * 2, out_specs=WHOLE, out_...  2.02 us
  transfers between devices with their start and end apart: 12, of which 3 were waited for; matrix products, arithmetic and copies ran while one was open for 0% of the time, Pallas kernels for 19%

profile of v2, /device:TPU:2, one launch (start us, length us, event | category | flops | bytes accessed | tf_op | source)
XLA Modules:
  0.0 85.8 jit_solution(17132579601359883862)
XLA Ops:
  0.6 0.0 copy-start
  0.7 0.9 %copy-done = bf16[128,768]{1,0:T(8,128)(2,1)S(1)} copy-done((bf16[128,768]{1,0:T(8,128)(2,1)S(1)}, bf16[128,768]{1,0:T(8,128)(2,1)}, u32[]{:S(2)}) %copy-start) | copy-done | bytes 196632
  1.6 0.1 add_add_fusion
  1.6 0.0 copy-start.1
  1.7 22.3 %all_to_all.10 = bf16[16,16,768]{2,1,0:T(8,128)(2,1)S(1)} all-to-all(bf16[16,16,768]{2,1,0:T(8,128)(2,1)S(1)} %broadcast_in_dim.2), channel_id=1, replica_groups={{0,1,2,3,4,5,6,7,8,9,10,11,12,13,14,15},{32,33,34,35,36,37,38,39,40,41,..., dimensions={0} | all-to-all | bytes 786432 | tf_op jit(solution)/shard_map/all_to_all | solution.py:54
  23.9 0.0 collective-permute-start.1
  23.9 1.2 %collective-permute-start = (bf16[256,768]{1,0:T(8,128)(2,1)S(1)}, bf16[256,768]{1,0:T(8,128)(2,1)S(1)}, u32[]{:S(2)}, u32[]{:S(2)}) collective-permute-start(bf16[256,768]{1,0:T(8,128)(2,1)S(1)} %bitcast.35), channel_id=1, source_target_pairs={{0,32},{32,64},{64,96},{96,0},{1,33},{33,65},{65,97},{97,1},{2,34}... | collective-permute-start | bytes 1179656 | tf_op jit(solution)/shard_map/ppermute | solution.py:62
  25.1 0.9 %collective-permute-start.4 = (bf16[256,768]{1,0:T(8,128)(2,1)S(1)}, bf16[256,768]{1,0:T(8,128)(2,1)S(1)}, u32[]{:S(2)}, u32[]{:S(2)}) collective-permute-start(bf16[256,768]{1,0:T(8,128)(2,1)S(1)} %bitcast.36), channel_id=1, source_target_pairs={{0,96},{32,0},{64,32},{96,64},{1,97},{33,1},{65,33},{97,65},{2,98}... | collective-permute-start | bytes 1179656 | tf_op jit(solution)/shard_map/ppermute | solution.py:62
  26.0 2.1 %collective-permute-start.2 = (bf16[256,768]{1,0:T(8,128)(2,1)S(1)}, bf16[256,768]{1,0:T(8,128)(2,1)S(1)}, u32[]{:S(2)}, u32[]{:S(2)}) collective-permute-start(bf16[256,768]{1,0:T(8,128)(2,1)S(1)} %bitcast.37), channel_id=1, source_target_pairs={{0,64},{32,96},{64,0},{96,32},{1,65},{33,97},{65,1},{97,33},{2,66}... | collective-permute-start | bytes 1179656 | tf_op jit(solution)/shard_map/ppermute | solution.py:62
  28.1 1.4 %copy-done.2 = bf16[1024,768]{1,0:T(8,128)(2,1)S(1)} copy-done((bf16[1024,768]{1,0:T(8,128)(2,1)S(1)}, bf16[1024,768]{1,0:T(8,128)(2,1)}, u32[]{:S(2)}) %copy-start.2) | copy-done | bytes 1572888
  29.5 1.1 %turned.1 = (bf16[2,384,1024]{2,1,0:T(8,128)(2,1)S(1)}, bf16[1024,768]{1,0:T(8,128)(2,1)S(1)}) custom-call(s32[3]{0:T(128)S(1)} %get-tuple-element.33.at_ref, bf16[1024,768]{1,0:T(8,128)(2,1)S(1)} %copy-done.2), custom_call_target="tpu_custom_call" | custom-call | flops 805306368 | bytes 5242880 | tf_op jit(solution)/shard_map/turned/pallas_call | solution.py:128
  30.6 0.0 collective-permute-done.1
  30.6 0.0 copy-done.1
  30.6 1.7 %errors.4 = (bf16[2,8,4,16,1024]{4,3,2,1,0:T(8,128)(2,1)S(1)}, bf16[2,8,4,16,1024]{4,3,2,1,0:T(8,128)(2,1)S(1)}) custom-call(s32[3]{0:T(128)S(1)} %get-tuple-element.33.at_ref, bf16[2,8,16,768]{3,2,1,0:T(8,128)(2,1)S(1)} %bitcast.38, bf16[2,8,16,768]{3,2,1,0:T(8,128)(2,1)S(1)} %bitcast.54, bf16[1024,768]{1,0:T(8,128)(2,1)S(1)} %get-tuple-element.37.w_ref, ...), custom_call_target="tpu_custom_call" | custom-call | flops 805306368 | bytes 5242880 | tf_op jit(solution)/shard_map/errors/pallas_call | solution.py:94
  32.3 0.0 collective-permute-done
  32.3 0.6 collective-permute-start.6
  32.9 0.0 collective-permute-done.4
  32.9 3.1 %collective-permute-start.5 = (bf16[256,768]{1,0:T(8,128)(2,1)S(1)}, bf16[256,768]{1,0:T(8,128)(2,1)S(1)}, u32[]{:S(2)}, u32[]{:S(2)}) collective-permute-start(bf16[256,768]{1,0:T(8,128)(2,1)S(1)} %collective-permute-done.4), channel_id=1, source_target_pairs={{0,16},{16,0},{1,17},{17,1},{2,18},{18,2},{3,19},{19,3},{4,20},{20... | collective-permute-start | bytes 1179656 | tf_op jit(solution)/shard_map/ppermute | solution.py:66
  36.1 2.0 %collective-permute-done.2 = bf16[256,768]{1,0:T(8,128)(2,1)S(1)} collective-permute-done((bf16[256,768]{1,0:T(8,128)(2,1)S(1)}, bf16[256,768]{1,0:T(8,128)(2,1)S(1)}, u32[]{:S(2)}, u32[]{:S(2)}) %collective-permute-start.2) | collective-permute-done | bytes 393248 | tf_op jit(solution)/shard_map/ppermute | solution.py:62
  38.1 0.0 collective-permute-start.3
  38.1 0.0 collective-permute-done.6
  38.1 1.7 %errors.5 = (bf16[2,8,4,16,1024]{4,3,2,1,0:T(8,128)(2,1)S(1)}, bf16[2,8,4,16,1024]{4,3,2,1,0:T(8,128)(2,1)S(1)}) custom-call(s32[3]{0:T(128)S(1)} %get-tuple-element.33.at_ref, bf16[2,8,16,768]{3,2,1,0:T(8,128)(2,1)S(1)} %bitcast.40, bf16[2,8,16,768]{3,2,1,0:T(8,128)(2,1)S(1)} %bitcast.46, ...), custom_call_target="tpu_custom_call", output_to_operand_aliasing={{0}: (5, {}), {1}: (6, {})} | custom-call | flops 805306368 | bytes 5242880 | tf_op jit(solution)/shard_map/errors/pallas_call | solution.py:94
  39.8 0.0 collective-permute-done.5
  39.8 1.7 %errors.6 = (bf16[2,8,4,16,1024]{4,3,2,1,0:T(8,128)(2,1)S(1)}, bf16[2,8,4,16,1024]{4,3,2,1,0:T(8,128)(2,1)S(1)}) custom-call(s32[3]{0:T(128)S(1)} %get-tuple-element.33.at_ref, bf16[2,8,16,768]{3,2,1,0:T(8,128)(2,1)S(1)} %bitcast.42, bf16[2,8,16,768]{3,2,1,0:T(8,128)(2,1)S(1)} %bitcast.48, ...), custom_call_target="tpu_custom_call", output_to_operand_aliasing={{0}: (5, {}), {1}: (6, {})} | custom-call | flops 805306368 | bytes 5242880 | tf_op jit(solution)/shard_map/errors/pallas_call | solution.py:94
  41.5 0.0 collective-permute-done.3
  41.6 1.7 %errors.7 = (bf16[2,8,4,16,1024]{4,3,2,1,0:T(8,128)(2,1)S(1)}, bf16[2,8,4,16,1024]{4,3,2,1,0:T(8,128)(2,1)S(1)}) custom-call(s32[3]{0:T(128)S(1)} %get-tuple-element.33.at_ref, bf16[2,8,16,768]{3,2,1,0:T(8,128)(2,1)S(1)} %bitcast.44, bf16[2,8,16,768]{3,2,1,0:T(8,128)(2,1)S(1)} %bitcast.50, ...), custom_call_target="tpu_custom_call", output_to_operand_aliasing={{0}: (5, {}), {1}: (6, {})} | custom-call | flops 805306368 | bytes 5242880 | tf_op jit(solution)/shard_map/errors/pallas_call | solution.py:94
  43.3 1.0 %theirs.3 = bf16[2,384,512]{2,1,0:T(8,128)(2,1)S(1)} custom-call(bf16[2,384,1024]{2,1,0:T(8,128)(2,1)S(1)} %get-tuple-element.41.wt_ref, bf16[1024,1024]{1,0:T(8,128)(2,1)S(1)} %bitcast.30), custom_call_target="tpu_custom_call" | custom-call | flops 805306368 | bytes 4194304 | tf_op jit(solution)/shard_map/theirs/pallas_call | solution.py:150
  44.3 0.6 collective-permute-start.8
  44.9 1.0 %theirs.2 = bf16[2,384,512]{2,1,0:T(8,128)(2,1)S(1)} custom-call(bf16[2,384,1024]{2,1,0:T(8,128)(2,1)S(1)} %get-tuple-element.41.wt_ref, bf16[1024,1024]{1,0:T(8,128)(2,1)S(1)} %bitcast.27), custom_call_target="tpu_custom_call" | custom-call | flops 805306368 | bytes 4194304 | tf_op jit(solution)/shard_map/theirs/pallas_call | solution.py:150
  45.9 0.3 collective-permute-start.7
  46.2 1.8 %mine.1 = f32[2,2,384,512]{3,2,1,0:T(8,128)S(1)} custom-call(bf16[2,384,1024]{2,1,0:T(8,128)(2,1)S(1)} %get-tuple-element.41.wt_ref, bf16[1024,1024]{1,0:T(8,128)(2,1)S(1)} %bitcast.28, bf16[1024,1024]{1,0:T(8,128)(2,1)S(1)} %bitcast.31), custom_call_target="tpu_custom_call" | custom-call | flops 1610612736 | bytes 8388608 | tf_op jit(solution)/shard_map/mine/pallas_call | solution.py:171
  48.0 0.0 collective-permute-done.8
  48.1 0.4 collective-permute-done.7
  48.5 0.8 join.1
  49.3 0.7 collective-permute-start.10
  50.0 1.2 %collective-permute-start.11 = (bf16[4,48,1024]{2,1,0:T(8,128)(2,1)S(1)}, bf16[4,48,1024]{2,1,0:T(8,128)(2,1)S(1)}, u32[]{:S(2)}, u32[]{:S(2)}) collective-permute-start(bf16[4,48,1024]{2,1,0:T(8,128)(2,1)S(1)} %get-tuple-element.53), channel_id=1, source_target_pairs={{0,64},{32,96},{64,0},{96,32},{1,65},{33,97},{65,1},{97,33},{2,66}... | collective-permute-start | bytes 1179656 | tf_op jit(solution)/shard_map/ppermute | solution.py:62
  51.2 2.5 %collective-permute-start.9 = (bf16[4,48,1024]{2,1,0:T(8,128)(2,1)S(1)}, bf16[4,48,1024]{2,1,0:T(8,128)(2,1)S(1)}, u32[]{:S(2)}, u32[]{:S(2)}) collective-permute-start(bf16[4,48,1024]{2,1,0:T(8,128)(2,1)S(1)} %get-tuple-element.51), channel_id=1, source_target_pairs={{0,32},{32,64},{64,96},{96,0},{1,33},{33,65},{65,97},{97,1},{2,34}... | collective-permute-start | bytes 1179656 | tf_op jit(solution)/shard_map/ppermute | solution.py:62
  53.7 0.7 by_block.2
  54.4 0.0 copy-start.3
  54.4 0.7 by_block.3
  55.1 0.7 copy-done.3
  55.8 5.8 %update.1 = (bf16[1024,768]{1,0:T(8,128)(2,1)}, bf16[1024,768]{1,0:T(8,128)(2,1)}) custom-call(bf16[1024,1024]{1,0:T(8,128)(2,1)S(1)} %bitcast.29, bf16[1024,1024]{1,0:T(8,128)(2,1)S(1)} %bitcast.32, bf16[1024,768]{1,0:T(8,128)(2,1)S(1)} %bitcast.52, bf16[1024,768]{1,0:T(8,128)(2,1)S(1)} %bitcast.53, bf16[1024,768]{1,0:T(8,128)(2,1)S(1)} %get-tuple-element.37.w_ref, ...), custom_call_target="tpu_custom_call" | custom-call | flops 3221225472 | bytes 12582912 | tf_op jit(solution)/shard_map/update/pallas_call | solution.py:271
  61.7 0.0 collective-permute-done.10.refs_2_
  61.7 0.0 collective-permute-done.11.refs_3_
  61.7 1.8 %collective-permute-done.9.refs_1_ = bf16[4,48,1024]{2,1,0:T(8,128)(2,1)S(1)} collective-permute-done((bf16[4,48,1024]{2,1,0:T(8,128)(2,1)S(1)}, bf16[4,48,1024]{2,1,0:T(8,128)(2,1)S(1)}, u32[]{:S(2)}, u32[]{:S(2)}) %collective-permute-start.9) | collective-permute-done | bytes 393248 | tf_op jit(solution)/shard_map/ppermute | solution.py:62
  63.5 0.3 large_total.1
  63.8 20.8 %all_to_all.11.u_ref = bf16[32,48,128]{2,1,0:T(8,128)(2,1)S(1)} all-to-all(bf16[32,48,128]{2,1,0:T(8,128)(2,1)S(1)} %large_total.1), channel_id=1, replica_groups={{0,1,2,3,4,5,6,7,8,9,10,11,12,13,14,15,128,129,130,131,132,133,134,135,..., dimensions={0} | all-to-all | bytes 786432 | tf_op jit(solution)/shard_map/all_to_all | solution.py:54
  84.6 1.3 %small_total.1 = bf16[48,128]{1,0:T(8,128)(2,1)} custom-call(s32[3]{0:T(128)S(1)} %get-tuple-element.33.at_ref, bf16[32,48,128]{2,1,0:T(8,128)(2,1)S(1)} %all_to_all.11.u_ref), custom_call_target="tpu_custom_call" | custom-call | flops 262144 | bytes 524288 | tf_op jit(solution)/shard_map/small_total/pallas_call | solution.py:248
  (3 shorter events, 0.0 us)
Async XLA Ops:
  0.6 0.9 %copy-start = (bf16[128,768]{1,0:T(8,128)(2,1)S(1)}, bf16[128,768]{1,0:T(8,128)(2,1)}, u32[]{:S(2)}) copy-start(bf16[128,768]{1,0:T(8,128)(2,1)} %param.4) | copy-start | bytes 589828
  1.6 28.9 %copy-start.1 = (bf16[2048,1024]{1,0:T(8,128)(2,1)S(1)}, bf16[2048,1024]{1,0:T(8,128)(2,1)}, u32[]{:S(2)}) copy-start(bf16[2048,1024]{1,0:T(8,128)(2,1)} %param.7) | copy-start | bytes 12582916
  23.9 6.6 %collective-permute-start.1 = (bf16[256,768]{1,0:T(8,128)(2,1)S(1)}, bf16[256,768]{1,0:T(8,128)(2,1)S(1)}, u32[]{:S(2)}, u32[]{:S(2)}) collective-permute-start(bf16[256,768]{1,0:T(8,128)(2,1)S(1)} %bitcast.34), channel_id=1, source_target_pairs={{0,16},{16,0},{1,17},{17,1},{2,18},{18,2},{3,19},{19,3},{4,20},{20... | collective-permute-start | bytes 1179656 | tf_op jit(solution)/shard_map/ppermute | solution.py:66
  23.9 8.4 %collective-permute-start = (bf16[256,768]{1,0:T(8,128)(2,1)S(1)}, bf16[256,768]{1,0:T(8,128)(2,1)S(1)}, u32[]{:S(2)}, u32[]{:S(2)}) collective-permute-start(bf16[256,768]{1,0:T(8,128)(2,1)S(1)} %bitcast.35), channel_id=1, source_target_pairs={{0,32},{32,64},{64,96},{96,0},{1,33},{33,65},{65,97},{97,1},{2,34}... | collective-permute-start | bytes 1179656 | tf_op jit(solution)/shard_map/ppermute | solution.py:62
  25.1 7.8 %collective-permute-start.4 = (bf16[256,768]{1,0:T(8,128)(2,1)S(1)}, bf16[256,768]{1,0:T(8,128)(2,1)S(1)}, u32[]{:S(2)}, u32[]{:S(2)}) collective-permute-start(bf16[256,768]{1,0:T(8,128)(2,1)S(1)} %bitcast.36), channel_id=1, source_target_pairs={{0,96},{32,0},{64,32},{96,64},{1,97},{33,1},{65,33},{97,65},{2,98}... | collective-permute-start | bytes 1179656 | tf_op jit(solution)/shard_map/ppermute | solution.py:62
  26.0 12.1 %collective-permute-start.2 = (bf16[256,768]{1,0:T(8,128)(2,1)S(1)}, bf16[256,768]{1,0:T(8,128)(2,1)S(1)}, u32[]{:S(2)}, u32[]{:S(2)}) collective-permute-start(bf16[256,768]{1,0:T(8,128)(2,1)S(1)} %bitcast.37), channel_id=1, source_target_pairs={{0,64},{32,96},{64,0},{96,32},{1,65},{33,97},{65,1},{97,33},{2,66}... | collective-permute-start | bytes 1179656 | tf_op jit(solution)/shard_map/ppermute | solution.py:62
  28.1 1.4 %copy-start.2 = (bf16[1024,768]{1,0:T(8,128)(2,1)S(1)}, bf16[1024,768]{1,0:T(8,128)(2,1)}, u32[]{:S(2)}) copy-start(bf16[1024,768]{1,0:T(8,128)(2,1)} %w_ref) | copy-start | bytes 4718596
  32.3 5.7 %collective-permute-start.6 = (bf16[256,768]{1,0:T(8,128)(2,1)S(1)}, bf16[256,768]{1,0:T(8,128)(2,1)S(1)}, u32[]{:S(2)}, u32[]{:S(2)}) collective-permute-start(bf16[256,768]{1,0:T(8,128)(2,1)S(1)} %collective-permute-done), channel_id=1, source_target_pairs={{0,16},{16,0},{1,17},{17,1},{2,18},{18,2},{3,19},{19,3},{4,20},{20... | collective-permute-start | bytes 1179656 | tf_op jit(solution)/shard_map/ppermute | solution.py:66
  32.9 6.9 %collective-permute-start.5 = (bf16[256,768]{1,0:T(8,128)(2,1)S(1)}, bf16[256,768]{1,0:T(8,128)(2,1)S(1)}, u32[]{:S(2)}, u32[]{:S(2)}) collective-permute-start(bf16[256,768]{1,0:T(8,128)(2,1)S(1)} %collective-permute-done.4), channel_id=1, source_target_pairs={{0,16},{16,0},{1,17},{17,1},{2,18},{18,2},{3,19},{19,3},{4,20},{20... | collective-permute-start | bytes 1179656 | tf_op jit(solution)/shard_map/ppermute | solution.py:66
  38.1 3.5 %collective-permute-start.3 = (bf16[256,768]{1,0:T(8,128)(2,1)S(1)}, bf16[256,768]{1,0:T(8,128)(2,1)S(1)}, u32[]{:S(2)}, u32[]{:S(2)}) collective-permute-start(bf16[256,768]{1,0:T(8,128)(2,1)S(1)} %collective-permute-done.2), channel_id=1, source_target_pairs={{0,16},{16,0},{1,17},{17,1},{2,18},{18,2},{3,19},{19,3},{4,20},{20... | collective-permute-start | bytes 1179656 | tf_op jit(solution)/shard_map/ppermute | solution.py:66
  44.3 3.7 %collective-permute-start.8 = (bf16[2,384,512]{2,1,0:T(8,128)(2,1)S(1)}, bf16[2,384,512]{2,1,0:T(8,128)(2,1)S(1)}, u32[]{:S(2)}, u32[]{:S(2)}) collective-permute-start(bf16[2,384,512]{2,1,0:T(8,128)(2,1)S(1)} %theirs.3), channel_id=1, source_target_pairs={{0,16},{16,0},{1,17},{17,1},{2,18},{18,2},{3,19},{19,3},{4,20},{20... | collective-permute-start | bytes 2359304 | tf_op jit(solution)/shard_map/ppermute | solution.py:66
  45.9 2.6 %collective-permute-start.7 = (bf16[2,384,512]{2,1,0:T(8,128)(2,1)S(1)}, bf16[2,384,512]{2,1,0:T(8,128)(2,1)S(1)}, u32[]{:S(2)}, u32[]{:S(2)}) collective-permute-start(bf16[2,384,512]{2,1,0:T(8,128)(2,1)S(1)} %theirs.2), channel_id=1, source_target_pairs={{0,16},{16,0},{1,17},{17,1},{2,18},{18,2},{3,19},{19,3},{4,20},{20... | collective-permute-start | bytes 2359304 | tf_op jit(solution)/shard_map/ppermute | solution.py:66
  49.3 12.3 %collective-permute-start.10 = (bf16[4,48,1024]{2,1,0:T(8,128)(2,1)S(1)}, bf16[4,48,1024]{2,1,0:T(8,128)(2,1)S(1)}, u32[]{:S(2)}, u32[]{:S(2)}) collective-permute-start(bf16[4,48,1024]{2,1,0:T(8,128)(2,1)S(1)} %get-tuple-element.52), channel_id=1, source_target_pairs={{0,96},{32,0},{64,32},{96,64},{1,97},{33,1},{65,33},{97,65},{2,98}... | collective-permute-start | bytes 1179656 | tf_op jit(solution)/shard_map/ppermute | solution.py:62
  50.0 11.7 %collective-permute-start.11 = (bf16[4,48,1024]{2,1,0:T(8,128)(2,1)S(1)}, bf16[4,48,1024]{2,1,0:T(8,128)(2,1)S(1)}, u32[]{:S(2)}, u32[]{:S(2)}) collective-permute-start(bf16[4,48,1024]{2,1,0:T(8,128)(2,1)S(1)} %get-tuple-element.53), channel_id=1, source_target_pairs={{0,64},{32,96},{64,0},{96,32},{1,65},{33,97},{65,1},{97,33},{2,66}... | collective-permute-start | bytes 1179656 | tf_op jit(solution)/shard_map/ppermute | solution.py:62
  51.2 12.3 %collective-permute-start.9 = (bf16[4,48,1024]{2,1,0:T(8,128)(2,1)S(1)}, bf16[4,48,1024]{2,1,0:T(8,128)(2,1)S(1)}, u32[]{:S(2)}, u32[]{:S(2)}) collective-permute-start(bf16[4,48,1024]{2,1,0:T(8,128)(2,1)S(1)} %get-tuple-element.51), channel_id=1, source_target_pairs={{0,32},{32,64},{64,96},{96,0},{1,33},{33,65},{65,97},{97,1},{2,34}... | collective-permute-start | bytes 1179656 | tf_op jit(solution)/shard_map/ppermute | solution.py:62
  54.4 1.4 %copy-start.3 = (bf16[1024,768]{1,0:T(8,128)(2,1)S(1)}, bf16[1024,768]{1,0:T(8,128)(2,1)}, u32[]{:S(2)}) copy-start(bf16[1024,768]{1,0:T(8,128)(2,1)} %m_ref.1) | copy-start | bytes 4718596
